TPU v7x, 32 devices: a whole 2x2x4 slice. The times are simulated.
32 devices in a mesh: dp: 4 (over z), sp: 8 (over y, x, core).
Axes of the slice: x: 2, y: 2, z: 4, core: 2. Of those that a mesh axis runs over, the one named last changes fastest.
Arguments:
- x_prompt: bfloat16 [48, 1024, 2048], P('dp', 'sp'), parts along dimension 0
- ln_attn_w: float32 [2048], replicated
- ln_attn_b: float32 [2048], replicated
- ln_mlp_w: float32 [2048], replicated
- ln_mlp_b: float32 [2048], replicated
- w_qkv: bfloat16 [2048, 16, 3, 128], replicated
- w_out: bfloat16 [2048, 2048], replicated
- w_up: bfloat16 [2048, 8192], replicated
- w_down: bfloat16 [8192, 2048], replicated
Outputs:
- output 1: bfloat16 [48, 1024, 2048], P('dp', 'sp'), parts along dimension 0
- output 2: bfloat16 [48, 16, 1024, 128], P('dp', 'sp'), parts along dimension 0
- output 3: bfloat16 [48, 16, 1024, 128], P('dp', 'sp'), parts along dimension 0
There are 4 independent parts. A program takes and returns all parts, laid end to end along the dimension named above; an argument that names none is the same for every part.
All inputs are finite; a program needn't handle non-finite values.
Results may differ from a plain program's by a relative error of at most 0.0040455.
Values are sent between devices in bfloat16 or wider.
A program may use at most 1 GiB of HBM per device.

v0:
```python
import functools

import jax
import jax.numpy as jnp
import numpy as np
from jax import lax
from jax.experimental import pallas as pl
from jax.experimental.pallas import tpu as pltpu
from jax.sharding import PartitionSpec as P

LN_EPS = 1e-5
ROPE_BASE = 10000.0
LOG2E = 1.4426950408889634
N_CHUNKS = 6
UP_TILE = 512
QKV_HEADS = 8
Q_TILE = 256
FIRST = 2
LATE_STEPS = 2
RELAYED = 4
F32 = jnp.float32
BF16 = jnp.bfloat16


def rope_tables(positions, head_dim):
    half_dim = head_dim // 2
    inv_freq = np.float32(ROPE_BASE) ** (np.float32(-2.0) * np.arange(half_dim, dtype=np.float32) / np.float32(head_dim))
    angles = np.arange(positions, dtype=np.float32)[:, None] * inv_freq[None, :]
    cos_t, sin_t = np.cos(angles.astype(np.float64)), np.sin(angles.astype(np.float64))
    wide = lambda a, b: jnp.asarray(np.concatenate([a, b], -1).astype(np.float32))
    return wide(cos_t, cos_t), wide(-sin_t, sin_t)


def causal_head(q, k, v, write):
    seq, head_dim = k.shape
    scale = LOG2E * head_dim**-0.5
    keys = lax.broadcasted_iota(jnp.int32, (Q_TILE, Q_TILE), 0)
    queries = lax.broadcasted_iota(jnp.int32, (Q_TILE, Q_TILE), 1)
    for i in range(q.shape[0] // Q_TILE):
        lo = seq - q.shape[0] + i * Q_TILE
        hi = lo + Q_TILE
        q_i = q[i * Q_TILE : (i + 1) * Q_TILE]
        scores = lax.dot_general(k[:hi], q_i, (((1,), (1,)), ((), ())), preferred_element_type=F32)
        diag = jnp.where(keys <= queries, scores[lo:], -1e30)
        scores = jnp.concatenate([scores[:lo], diag], axis=0) if lo else diag
        prob = jnp.exp2((scores - jnp.max(scores, axis=0, keepdims=True)) * scale)
        prob = (prob * (1.0 / jnp.sum(prob, axis=0, keepdims=True))).astype(BF16)
        out = lax.dot_general(prob, v[:hi], (((0,), (0,)), ((), ())), preferred_element_type=F32)
        write(i, out.astype(BF16))


def layer_kernel(
    n,
    x_hbm,
    cos_hbm,
    sin_hbm,
    ln_aw_hbm,
    ln_ab_hbm,
    ln_mw_hbm,
    ln_mb_hbm,
    w_qkv,
    w_out,
    w_up,
    w_down,
    h_mlp,
    recv,
    send,
    ctx_send,
    near,
    ctx_near,
    relay,
    acc,
    ctx_rows,
    ln_buf,
    x_sem,
    ln_sem,
    w_sem,
    bounce_sem,
    own_sem,
    up_sem,
    down_sem,
    qkv_sem,
    near_sem,
    send_sem,
    recv_sem,
    ctx_send_sem,
    ctx_recv_sem,
    near_send_sem,
    near_recv_sem,
    ctx_near_send_sem,
    ctx_near_recv_sem,
    relay_recv_sem,
    relay_send_sem,
):
    me = lax.axis_index("sp")
    n_batch, _, heads, seq_dev, head_dim = send.shape[1:]
    cols = heads * head_dim
    width = x_hbm.shape[1]
    nb = n_batch // N_CHUNKS
    rows = nb * seq_dev
    ffn = w_up.shape[1]
    dests = QKV_HEADS // heads
    parts = n // dests
    blocks = 3 * parts

    def peer(step):
        return lax.bitwise_xor(me, step)

    def rows_of(chunk, first, count=1):
        return ctx_rows.at[pl.ds(chunk * nb, nb), :, pl.ds(pl.multiple_of(first * cols, cols), count * cols)]

    def put(chunk, kind, to, frm):
        bs = pl.ds(chunk * nb, nb)
        return pltpu.make_async_remote_copy(
            src_ref=send.at[kind, bs, to],
            dst_ref=recv.at[kind, bs, :, frm],
            send_sem=send_sem.at[chunk],
            recv_sem=recv_sem.at[chunk, kind],
            device_id={"sp": to},
            device_id_type=pl.DeviceIdType.MESH,
        )

    def put_ctx(chunk, to, frm):
        bs = pl.ds(chunk * nb, nb)
        return pltpu.make_async_remote_copy(
            src_ref=ctx_send.at[bs, to],
            dst_ref=rows_of(chunk, frm),
            send_sem=ctx_send_sem.at[chunk],
            recv_sem=ctx_recv_sem.at[chunk, frm // FIRST],
            device_id={"sp": to},
            device_id_type=pl.DeviceIdType.MESH,
        )

    def put_relay(chunk, to, slot):
        bs = pl.ds(chunk * nb, nb)
        return pltpu.make_async_remote_copy(
            src_ref=ctx_send.at[bs, to],
            dst_ref=relay.at[bs, slot],
            send_sem=ctx_send_sem.at[chunk],
            recv_sem=relay_recv_sem.at[chunk],
            device_id={"sp": to - FIRST},
            device_id_type=pl.DeviceIdType.MESH,
        )

    def forward(chunk, slot):
        bs = pl.ds(chunk * nb, nb)
        return pltpu.make_async_remote_copy(
            src_ref=relay.at[bs, slot],
            dst_ref=rows_of(chunk, 2 * FIRST + slot),
            send_sem=relay_send_sem.at[chunk],
            recv_sem=ctx_recv_sem.at[chunk, 2],
            device_id={"sp": me + FIRST},
            device_id_type=pl.DeviceIdType.MESH,
        )

    def put_near(chunk, kind):
        bs = pl.ds(chunk * nb, nb)
        return pltpu.make_async_remote_copy(
            src_ref=send.at[kind, bs, pl.ds((1 - me) * dests, dests)],
            dst_ref=near.at[kind, bs],
            send_sem=near_send_sem.at[chunk],
            recv_sem=near_recv_sem.at[chunk],
            device_id={"sp": 1 - me},
            device_id_type=pl.DeviceIdType.MESH,
        )

    def put_ctx_near(chunk):
        bs = pl.ds(chunk * nb, nb)
        return pltpu.make_async_remote_copy(
            src_ref=ctx_near.at[bs, 1 - me],
            dst_ref=rows_of(chunk, me * dests, dests),
            send_sem=ctx_near_send_sem.at[chunk],
            recv_sem=ctx_near_recv_sem.at[chunk],
            device_id={"sp": 1 - me},
            device_id_type=pl.DeviceIdType.MESH,
        )

    def drain(ref, sem):
        pltpu.make_async_copy(ref, ref, sem).wait()

    is_first = me < FIRST
    later_on = jnp.logical_not(is_first)

    def each_peer(do, lowest=0):
        for other in range(lowest, n):
            pl.when(other != me)(functools.partial(do, other))

    def qkv_phase(x_buf, h_attn, w_nat, w_cols, out_buf, own, cos_ref, sin_ref):
        mine = pl.ds(pl.multiple_of(me * seq_dev, seq_dev), seq_dev)
        get_cos = pltpu.make_async_copy(cos_hbm.at[mine], cos_ref, own_sem.at[3])
        get_sin = pltpu.make_async_copy(sin_hbm.at[mine], sin_ref, own_sem.at[4])

        def get_x(chunk):
            return pltpu.make_async_copy(x_hbm.at[pl.ds(chunk * rows, rows)], x_buf, x_sem)

        def get_w(half):
            block, slot = half // 2, lax.rem(half, 2)
            src = w_qkv.at[
                pl.ds(slot * (width // 2), width // 2),
                block // parts,
                pl.ds(lax.rem(block, parts) * QKV_HEADS, QKV_HEADS),
            ]
            return pltpu.make_async_copy(src, w_nat.at[slot], w_sem.at[slot])

        def bounce(step):
            slot, block = lax.rem(step, 2), lax.rem(step, blocks)
            dst = send.at[
                block // parts, pl.ds(step // blocks * nb, nb), pl.ds(lax.rem(block, parts) * dests, dests)
            ]
            return pltpu.make_async_copy(out_buf.at[slot], dst, bounce_sem.at[slot])

        def put_own(chunk, kind):
            dst = recv.at[kind, pl.ds(chunk * nb, nb), :, me]
            return pltpu.make_async_copy(own.at[kind], dst, own_sem.at[kind])

        def send_block(step):
            bounce(step).wait()
            block = lax.rem(step, blocks)
            for d in range(dests):
                to = lax.rem(block, parts) * dests + lax.rem(me + d, dests)

                @pl.when((to != me) & jnp.logical_not(is_first & (block < parts)))
                def _():
                    put(step // blocks, block // parts, to, me).start()

            @pl.when(is_first & (lax.rem(block, parts) == 1 - me))
            def _():
                put_near(step // blocks, block // parts).start()

        ln_hbm = (ln_aw_hbm, ln_ab_hbm, ln_mw_hbm, ln_mb_hbm)
        get_ln = [pltpu.make_async_copy(p, ln_buf.at[i], ln_sem.at[i]) for i, p in enumerate(ln_hbm)]
        ln_aw, ln_ab, ln_mw, ln_mb = (ln_buf.at[i] for i in range(4))
        get_x(0).start()
        for copy in get_ln:
            copy.start()
        get_w(0).start()
        get_w(1).start()
        get_cos.start()
        get_sin.start()
        barrier = pltpu.get_barrier_semaphore()
        for step in range(1, n):
            pl.semaphore_signal(
                barrier, inc=1, device_id={"sp": peer(step)}, device_id_type=pl.DeviceIdType.MESH
            )

        @pl.loop(0, N_CHUNKS * blocks)
        def _(step):
            chunk, block = step // blocks, lax.rem(step, blocks)
            kind, part = block // parts, lax.rem(block, parts)
            slot = lax.rem(step, 2)

            @pl.when(block == 0)
            def _():
                get_x(chunk).wait()

                @pl.when(chunk == 0)
                def _():
                    for copy in get_ln:
                        copy.wait()

                @pl.loop(0, nb)
                def _(i):
                    r = pl.ds(pl.multiple_of(i * seq_dev, seq_dev), seq_dev)
                    g = pl.ds(pl.multiple_of(chunk * rows + i * seq_dev, seq_dev), seq_dev)
                    xf = x_buf[r, :].astype(F32)
                    mean = jnp.sum(xf, axis=-1, keepdims=True) * (1.0 / width)
                    dev = xf - mean
                    var = jnp.sum(dev * dev, axis=-1, keepdims=True) * (1.0 / width)
                    unit = dev * lax.rsqrt(var + LN_EPS)
                    h_attn[r, :] = (unit * ln_aw[...] + ln_ab[...]).astype(BF16)
                    h_mlp[g, :] = (unit * ln_mw[...] + ln_mb[...]).astype(BF16)
                    acc[g, :] = xf

                @pl.when(chunk + 1 < N_CHUNKS)
                def _():
                    get_x(chunk + 1).start()

            @pl.when(chunk == 0)
            def _():
                @pl.when(block == 0)
                def _():
                    get_cos.wait()
                    get_sin.wait()

                @pl.loop(2 * block, 2 * block + 2)
                def _(half):
                    get_w(half).wait()

                    @pl.loop(0, width // 2 // 128)
                    def _(i):
                        r = pl.ds(pl.multiple_of(i * 128, 128), 128)
                        top = lax.rem(half, 2) * (width // 2)
                        to = pl.ds(pl.multiple_of(top + i * 128, 128), 128)
                        by_head = jnp.swapaxes(w_nat[lax.rem(half, 2), r].astype(F32), 0, 1)
                        for h in range(QKV_HEADS):
                            w_cols[block, to, h * head_dim : (h + 1) * head_dim] = by_head[h].astype(BF16)

                    @pl.when(half + 2 < 2 * blocks)
                    def _():
                        get_w(half + 2).start()

            for d in range(dests):
                cs = slice(d * heads * head_dim, (d + 1) * heads * head_dim)
                cols = jnp.dot(h_attn[...], w_cols[block, :, cs], preferred_element_type=F32)
                for h in range(heads):
                    for b in range(nb):
                        u = cols[b * seq_dev : (b + 1) * seq_dev, h * head_dim : (h + 1) * head_dim]
                        u = u.astype(BF16).astype(F32)
                        turned = u * cos_ref[...] + pltpu.roll(u, head_dim // 2, 1) * sin_ref[...]
                        out_buf[slot, b, d, h] = jnp.where(kind < 2, turned, u).astype(BF16)

            bounce(step).start()

            @pl.when(me // dests == part)
            def _():
                @pl.when(chunk > 0)
                def _():
                    put_own(chunk - 1, kind).wait()

                own[kind] = out_buf[slot, :, lax.rem(me, dests)]
                put_own(chunk, kind).start()

            @pl.when(step == 0)
            def _():
                pl.semaphore_wait(barrier, n - 1)

            @pl.when(chunk == 0)
            def _():
                send_block(step)

            @pl.when(step > blocks)
            def _():
                send_block(step - 1)

        send_block(N_CHUNKS * blocks - 1)
        for kind in range(3):
            put_own(N_CHUNKS - 1, kind).wait()

    pl.run_scoped(
        qkv_phase,
        pltpu.VMEM((rows, width), BF16),
        pltpu.VMEM((rows, width), BF16),
        pltpu.VMEM((2, width // 2, QKV_HEADS, head_dim), BF16),
        pltpu.VMEM((blocks, width, QKV_HEADS * head_dim), BF16),
        pltpu.VMEM((2, nb, dests, heads, seq_dev, head_dim), BF16),
        pltpu.VMEM((3, nb, heads, seq_dev, head_dim), BF16),
        pltpu.VMEM((seq_dev, head_dim), F32),
        pltpu.VMEM((seq_dev, head_dim), F32),
    )

    def rest(up_buf, down_buf, w_buf, qkv_buf, ctx_buf, both, near_buf):
        later = n - FIRST
        steps = ffn // UP_TILE

        def get_up(f):
            cols = pl.ds(pl.multiple_of(f * UP_TILE, UP_TILE), UP_TILE)
            slot = lax.rem(f, 2)
            return pltpu.make_async_copy(w_up.at[:, cols], up_buf.at[slot], up_sem.at[slot])

        def get_down(f):
            cols = pl.ds(pl.multiple_of(f * UP_TILE, UP_TILE), UP_TILE)
            slot = lax.rem(f, 2)
            return pltpu.make_async_copy(w_down.at[cols], down_buf.at[slot], down_sem.at[slot])

        def get_w_out():
            return pltpu.make_async_copy(w_out, w_buf, w_sem.at[0])

        def get_qkv(chunk, kind):
            return pltpu.make_async_copy(recv.at[kind, pl.ds(chunk * nb, nb)], qkv_buf.at[kind], qkv_sem.at[kind])

        def get_own_near(chunk, kind):
            src = send.at[kind, pl.ds(chunk * nb, nb), pl.ds(me * dests, dests)]
            return pltpu.make_async_copy(src, both.at[kind, :, :, :, me], near_sem.at[kind, 0])

        def get_other_near(chunk, kind):
            src = near.at[kind, pl.ds(chunk * nb, nb)]
            return pltpu.make_async_copy(src, both.at[kind, :, :, :, 1 - me], near_sem.at[kind, 1])

        def bounce_ctx(chunk):
            dst = ctx_send.at[pl.ds(chunk * nb, nb), pl.ds(FIRST, later)]
            return pltpu.make_async_copy(ctx_buf, dst, bounce_sem.at[0])

        def bounce_near(chunk):
            return pltpu.make_async_copy(near_buf, ctx_near.at[pl.ds(chunk * nb, nb)], bounce_sem.at[1])

        def send_ctx(chunk):
            bounce_ctx(chunk).wait()
            relays = (me // FIRST == 2) & (chunk < RELAYED)

            def one(other):
                if other // FIRST == 1:

                    @pl.when(relays)
                    def _():
                        put_relay(chunk, other, me - 2 * FIRST).start()

                    @pl.when(jnp.logical_not(relays))
                    def _():
                        put_ctx(chunk, other, me).start()

                else:
                    put_ctx(chunk, other, me).start()

            each_peer(one, FIRST)

        def send_near(chunk):
            bounce_near(chunk).wait()
            put_ctx_near(chunk).start()

        def pass_on(chunk):
            drain(relay.at[pl.ds(chunk * nb, nb)], relay_recv_sem.at[chunk])
            for slot in range(FIRST):
                forward(chunk, slot).start()

        def load_qkv(chunk):
            for kind in range(3):
                got = lambda count: recv.at[kind, pl.ds(chunk * nb, nb), :, pl.ds(0, count)]
                if kind:
                    drain(got(n - 1), recv_sem.at[chunk, kind])
                else:
                    pl.when(is_first)(lambda: drain(got(n - FIRST), recv_sem.at[chunk, kind]))
                    pl.when(later_on)(lambda: drain(got(n - FIRST - 1), recv_sem.at[chunk, kind]))
                get_qkv(chunk, kind).start()

            @pl.when(is_first)
            def _():
                drain(near.at[:, pl.ds(chunk * nb, nb)], near_recv_sem.at[chunk])
                for kind in range(3):
                    get_own_near(chunk, kind).start()
                    get_other_near(chunk, kind).start()

        get_up(0).start()
        get_down(0).start()
        get_w_out().start()

        @pl.loop(0, N_CHUNKS + 1)
        def _(chunk):
            early = steps - LATE_STEPS
            first = chunk * early // N_CHUNKS
            last = jnp.where(chunk < N_CHUNKS, (chunk + 1) * early // N_CHUNKS, steps)

            @pl.loop(first, last)
            def _(f):
                slot = lax.rem(f, 2)

                @pl.when(f + 1 < steps)
                def _():
                    get_up(f + 1).start()
                    get_down(f + 1).start()

                @pl.when((f == last - 1) & (chunk < N_CHUNKS - 1))
                def _():
                    load_qkv(chunk)

                get_up(f).wait()
                get_down(f).wait()
                for r in range(n_batch * seq_dev // 512):
                    rs = pl.ds(r * 512, 512)
                    up = jnp.dot(h_mlp[rs, :], up_buf[slot], preferred_element_type=F32)
                    hid = (0.5 * up * (1.0 + lax.erf(up * 0.5**0.5))).astype(BF16)
                    acc[rs, :] += jnp.dot(hid, down_buf[slot], preferred_element_type=F32)

                @pl.when((f == first) & (chunk > 0))
                def _():
                    @pl.when(chunk < N_CHUNKS)
                    def _():
                        send_ctx(chunk - 1)

                    @pl.when(is_first)
                    def _():
                        send_near(chunk - 1)

                @pl.when(is_first & (chunk == N_CHUNKS))
                def _():
                    first_relay = 1 + (f - first) * 2

                    @pl.loop(first_relay, jnp.minimum(jnp.where(f == steps - 1, RELAYED, first_relay + 2), RELAYED))
                    def _(c):
                        pass_on(c)

            @pl.when(chunk < N_CHUNKS)
            def _():
                @pl.when(chunk == N_CHUNKS - 1)
                def _():
                    load_qkv(chunk)

                for kind in range(3):
                    get_qkv(chunk, kind).wait()
                for b in range(nb):
                    for h in range(heads):
                        q = qkv_buf[0, b, h, FIRST:].reshape(later * seq_dev, head_dim)
                        k, v = (qkv_buf[t, b, h].reshape(n * seq_dev, head_dim) for t in (1, 2))
                        per = Q_TILE // seq_dev

                        def write(i, out):
                            ctx_buf[b, i * per : (i + 1) * per, :, h * head_dim : (h + 1) * head_dim] = out.reshape(
                                per, seq_dev, head_dim
                            )

                        causal_head(q, k, v, write)
                bounce_ctx(chunk).start()

                @pl.when(later_on)
                def _():
                    rows_of(chunk, me)[...] = ctx_buf[:, me - FIRST]

                @pl.when(chunk == N_CHUNKS - 1)
                def _():
                    send_ctx(chunk)

                    @pl.when(is_first)
                    def _():
                        pass_on(0)

                @pl.when(is_first)
                def _():
                    for kind in range(3):
                        get_own_near(chunk, kind).wait()
                        get_other_near(chunk, kind).wait()

                    @pl.loop(0, nb)
                    def _(b):
                        for d in range(dests):
                            for h in range(heads):
                                q, k, v = (both[t, b, d, h].reshape(Q_TILE, head_dim) for t in range(3))

                                def write(i, out):
                                    col = (d * heads + h) * head_dim
                                    near_buf[b, :, :, col : col + head_dim] = out.reshape(
                                        FIRST, seq_dev, head_dim
                                    )

                                causal_head(q, k, v, write)

                    bounce_near(chunk).start()
                    rows_of(chunk, me * dests, dests)[...] = near_buf[:, me]

        get_w_out().wait()

        @pl.loop(0, N_CHUNKS)
        def _(turn):
            chunk = jnp.where(turn == 2, RELAYED, jnp.where((turn > 2) & (turn <= RELAYED), turn - 1, turn))

            g = pl.ds(pl.multiple_of(chunk * rows, rows), rows)
            pl.when(is_first)(lambda: put_ctx_near(chunk).wait_recv())
            for part in range(n // FIRST):
                home = me // FIRST
                source = jnp.where(part == 0, home, jnp.where(part <= home, part - 1, part))

                @pl.when(later_on)
                def _():
                    count = FIRST - (part == 0)
                    drain(rows_of(chunk, 0, count), ctx_recv_sem.at[chunk, source])

                span = pl.ds(pl.multiple_of(source * FIRST * cols, FIRST * cols), FIRST * cols)
                left = ctx_rows[pl.ds(chunk * nb, nb), :, span].reshape(rows, FIRST * cols)
                for c in range(0, width, 1024):
                    cs = slice(c, c + 1024)
                    total = acc[g, cs] + jnp.dot(left, w_buf[span, cs], preferred_element_type=F32)
                    if part < n // FIRST - 1:
                        acc[g, cs] = total
                    else:
                        h_mlp[g, cs] = total.astype(BF16)

    pl.run_scoped(
        rest,
        pltpu.VMEM((2, width, UP_TILE), BF16),
        pltpu.VMEM((2, UP_TILE, width), BF16),
        pltpu.VMEM((width, width), BF16),
        pltpu.VMEM((3, nb, heads, n, seq_dev, head_dim), BF16),
        pltpu.VMEM((nb, n - FIRST, seq_dev, cols), BF16),
        pltpu.VMEM((3, nb, dests, heads, FIRST, seq_dev, head_dim), BF16),
        pltpu.VMEM((nb, FIRST, seq_dev, dests * cols), BF16),
    )

    @pl.loop(0, N_CHUNKS)
    def _(chunk):
        bs = pl.ds(chunk * nb, nb)

        @pl.when(is_first)
        def _():
            drain(send.at[pl.ds(1, 2), bs, pl.ds(0, n - 1)], send_sem.at[chunk])
            drain(near.at[:, bs], near_send_sem.at[chunk])
            drain(ctx_send.at[bs, pl.ds(0, n - FIRST)], ctx_send_sem.at[chunk])
            drain(ctx_near.at[bs, 0], ctx_near_send_sem.at[chunk])
            pl.when(chunk < RELAYED)(lambda: drain(relay.at[bs], relay_send_sem.at[chunk]))

        @pl.when(later_on)
        def _():
            drain(send.at[:, bs, pl.ds(0, n - 1)], send_sem.at[chunk])
            drain(ctx_send.at[bs, pl.ds(0, n - FIRST - 1)], ctx_send_sem.at[chunk])


def store_kernel(y_ref, kv_hbm, y_hbm, k_hbm, v_hbm, buf, in_sem, out_sem, y_sem):
    n_batch = k_hbm.shape[0]
    y_out = pltpu.make_async_copy(y_ref, y_hbm, y_sem)
    pieces = [(t, b) for t in range(2) for b in range(n_batch)]
    get = [
        pltpu.make_async_copy(kv_hbm.at[1 + t, b], buf.at[t, b], in_sem.at[t, b]) for t, b in pieces
    ]
    put = [
        pltpu.make_async_copy(buf.at[t, b], (k_hbm, v_hbm)[t].at[b], out_sem.at[t, b]) for t, b in pieces
    ]
    for copy in get:
        copy.start()
    y_out.start()
    for got, going in zip(get, put):
        got.wait()
        going.start()
    for copy in put:
        copy.wait()
    y_out.wait()


def solution(mesh):
    n = mesh.shape["sp"]

    def local_layer(x_blk, ln_attn_w, ln_attn_b, ln_mlp_w, ln_mlp_b, w_qkv, w_out, w_up, w_down):
        n_batch, seq_dev, width = x_blk.shape
        groups, head_dim = w_qkv.shape[1], w_qkv.shape[3]
        heads = groups // n
        nb = n_batch // N_CHUNKS
        rows = n_batch * seq_dev
        dests = QKV_HEADS // heads
        ffn = w_up.shape[1]
        cos_t, sin_t = rope_tables(n * seq_dev, head_dim)
        row = lambda p: p.reshape(1, width)
        anywhere = pl.BlockSpec(memory_space=pl.ANY)
        flops = 2 * rows * width * (3 * width + 2 * ffn) + 2 * rows * n * seq_dev * width * 2
        y_out, recv, *_ = pl.pallas_call(
            functools.partial(layer_kernel, n),
            out_shape=[
                pltpu.VMEM((rows, width), BF16),
                jax.ShapeDtypeStruct((3, n_batch, heads, n, seq_dev, head_dim), BF16),
                jax.ShapeDtypeStruct((3, n_batch, n, heads, seq_dev, head_dim), BF16),
                jax.ShapeDtypeStruct((n_batch, n, seq_dev, heads * head_dim), BF16),
                jax.ShapeDtypeStruct((3, n_batch, dests, heads, seq_dev, head_dim), BF16),
                jax.ShapeDtypeStruct((n_batch, FIRST, seq_dev, dests * heads * head_dim), BF16),
                jax.ShapeDtypeStruct((n_batch, FIRST, seq_dev, heads * head_dim), BF16),
            ],
            in_specs=[anywhere] * 11,
            out_specs=[pl.BlockSpec(memory_space=pltpu.VMEM)] + [anywhere] * 6,
            scratch_shapes=[
                pltpu.VMEM((rows, width), F32),
                pltpu.VMEM((n_batch, seq_dev, width), BF16),
                pltpu.VMEM((4, 1, width), F32),
                pltpu.SemaphoreType.DMA,
                pltpu.SemaphoreType.DMA((4,)),
                pltpu.SemaphoreType.DMA((2,)),
                pltpu.SemaphoreType.DMA((2,)),
                pltpu.SemaphoreType.DMA((5,)),
                pltpu.SemaphoreType.DMA((2,)),
                pltpu.SemaphoreType.DMA((2,)),
                pltpu.SemaphoreType.DMA((3,)),
                pltpu.SemaphoreType.DMA((3, 2)),
                pltpu.SemaphoreType.DMA((N_CHUNKS,)),
                pltpu.SemaphoreType.DMA((N_CHUNKS, 3)),
                pltpu.SemaphoreType.DMA((N_CHUNKS,)),
                pltpu.SemaphoreType.DMA((N_CHUNKS, n // FIRST)),
                pltpu.SemaphoreType.DMA((N_CHUNKS,)),
                pltpu.SemaphoreType.DMA((N_CHUNKS,)),
                pltpu.SemaphoreType.DMA((N_CHUNKS,)),
                pltpu.SemaphoreType.DMA((N_CHUNKS,)),
                pltpu.SemaphoreType.DMA((N_CHUNKS,)),
                pltpu.SemaphoreType.DMA((N_CHUNKS,)),
            ],
            compiler_params=pltpu.CompilerParams(
                collective_id=0, has_side_effects=True, vmem_limit_bytes=57 * 2**20
            ),
            cost_estimate=pl.CostEstimate(flops=flops, bytes_accessed=3 * 10**8, transcendentals=10**7),
            name="layer",
        )(
            x_blk.reshape(rows, width),
            cos_t,
            sin_t,
            row(ln_attn_w),
            row(ln_attn_b),
            row(ln_mlp_w),
            row(ln_mlp_b),
            w_qkv.transpose(0, 2, 1, 3),
            w_out,
            w_up,
            w_down,
        )
        cache = jax.ShapeDtypeStruct((n_batch, heads, n, seq_dev, head_dim), BF16)
        y_out, k_cache, v_cache = pl.pallas_call(
            store_kernel,
            out_shape=[jax.ShapeDtypeStruct((rows, width), BF16), cache, cache],
            in_specs=[pl.BlockSpec(memory_space=pltpu.VMEM), pl.BlockSpec(memory_space=pltpu.HBM)],
            out_specs=[pl.BlockSpec(memory_space=pltpu.HBM)] * 3,
            scratch_shapes=[
                pltpu.VMEM((2, n_batch, heads, n, seq_dev, head_dim), BF16),
                pltpu.SemaphoreType.DMA((2, n_batch)),
                pltpu.SemaphoreType.DMA((2, n_batch)),
                pltpu.SemaphoreType.DMA,
            ],
            compiler_params=pltpu.CompilerParams(vmem_limit_bytes=56 * 2**20),
            cost_estimate=pl.CostEstimate(flops=10**6, bytes_accessed=3 * 10**7, transcendentals=0),
            name="store",
        )(y_out, recv)
        shape = (n_batch, heads, n * seq_dev, head_dim)
        return y_out.reshape(x_blk.shape), k_cache.reshape(shape), v_cache.reshape(shape)

    act_spec, cache_spec = P("dp", "sp", None), P("dp", "sp", None, None)
    return jax.shard_map(
        local_layer,
        mesh=mesh,
        in_specs=(act_spec,) + (P(),) * 8,
        out_specs=(act_spec, cache_spec, cache_spec),
        check_vma=False,
    )
```

profile of v0, /device:TPU:27, one launch (start us, length us, event | category | flops | bytes accessed | tf_op | source)
XLA Modules:
  0.0 277.6 jit_solution(14731015534799222068)
XLA Ops:
  0.6 259.9 %layer.1 = (bf16[1536,2048]{1,0:T(8,128)(2,1)S(1)}, bf16[3,12,2,8,128,128]{5,4,3,2,1,0:T(8,128)(2,1)}, bf16[3,12,8,2,128,128]{5,4,3,2,1,0:T(8,128)(2,1)}, bf16[1...) custom-call(bf16[1536,2048]{1,0:T(8,128)(2,1)} %bitcast.10, ...), custom_call_target="tpu_custom_call" | custom-call | flops 154618822656 | bytes 300000000 | tf_op jit(solution)/shard_map/layer/pallas_call | solution.py:630
  260.5 0.0 copy-start
  260.5 2.6 copy-done
  263.1 14.5 %store.1 = (bf16[1536,2048]{1,0:T(8,128)(2,1)}, bf16[12,2,8,128,128]{4,3,2,1,0:T(8,128)(2,1)}, bf16[12,2,8,128,128]{4,3,2,1,0:T(8,128)(2,1)}) custom-call(bf16[1536,2048]{1,0:T(8,128)(2,1)} %copy-done, bf16[3,12,2,8,128,128]{5,4,3,2,1,0:T(8,128)(2,1)} %get-tuple-element.9.kv_hbm), custom_call_target="tpu_custom_call" | custom-call | flops 1000000 | bytes 30000000 | tf_op jit(solution)/shard_map/store/pallas_call | solution.py:686
Async XLA Ops:
  260.5 2.6 copy-start
where the time goes:
time: 278 us
  Pallas kernels  274 us (99%)
    pallas_call x1, Pallas kernels, local_layer(): pl.pallas_call(functools.partial(layer_kernel, n), out_shape=[pltpu.VMEM(...  260 us
    pallas_call x1, Pallas kernels, local_layer(): pl.pallas_call(store_kernel, out_shape=[jax.ShapeDtypeStruct((rows, width...  14.5 us

commit v1 on v0

--- a/solution.py
+++ b/solution.py
@@ -686,7 +686,7 @@
         y_out, k_cache, v_cache = pl.pallas_call(
             store_kernel,
             out_shape=[jax.ShapeDtypeStruct((rows, width), BF16), cache, cache],
-            in_specs=[pl.BlockSpec(memory_space=pltpu.VMEM), pl.BlockSpec(memory_space=pltpu.HBM)],
+            in_specs=[anywhere] * 2,
             out_specs=[pl.BlockSpec(memory_space=pltpu.HBM)] * 3,
             scratch_shapes=[
                 pltpu.VMEM((2, n_batch, heads, n, seq_dev, head_dim), BF16),
@@ -694,7 +694,7 @@
                 pltpu.SemaphoreType.DMA((2, n_batch)),
                 pltpu.SemaphoreType.DMA,
             ],
-            compiler_params=pltpu.CompilerParams(vmem_limit_bytes=56 * 2**20),
+            compiler_params=pltpu.CompilerParams(vmem_limit_bytes=44 * 2**20),
             cost_estimate=pl.CostEstimate(flops=10**6, bytes_accessed=3 * 10**7, transcendentals=0),
             name="store",
         )(y_out, recv)

time: 278 us -> 272 us (0.978)
  no operation moved by 1% of the time
where the time goes in v1:
time: 272 us
  Pallas kernels  272 us (100%)
    pallas_call x1, Pallas kernels, local_layer(): pl.pallas_call(functools.partial(layer_kernel, n), out_shape=[pltpu.VMEM(...  260 us
    pallas_call x1, Pallas kernels, local_layer(): pl.pallas_call(store_kernel, out_shape=[jax.ShapeDtypeStruct((rows, width...  11.7 us

profile of v1, /device:TPU:27, one launch (start us, length us, event | category | flops | bytes accessed | tf_op | source)
XLA Modules:
  0.0 272.2 jit_solution(10820718729767944544)
XLA Ops:
  0.6 259.8 %layer.1 = (bf16[1536,2048]{1,0:T(8,128)(2,1)S(1)}, bf16[3,12,2,8,128,128]{5,4,3,2,1,0:T(8,128)(2,1)}, bf16[3,12,8,2,128,128]{5,4,3,2,1,0:T(8,128)(2,1)}, bf16[1...) custom-call(bf16[1536,2048]{1,0:T(8,128)(2,1)} %bitcast.10, ...), custom_call_target="tpu_custom_call" | custom-call | flops 154618822656 | bytes 300000000 | tf_op jit(solution)/shard_map/layer/pallas_call | solution.py:630
  260.5 11.7 %store.1 = (bf16[1536,2048]{1,0:T(8,128)(2,1)}, bf16[12,2,8,128,128]{4,3,2,1,0:T(8,128)(2,1)}, bf16[12,2,8,128,128]{4,3,2,1,0:T(8,128)(2,1)}) custom-call(bf16[1536,2048]{1,0:T(8,128)(2,1)S(1)} %get-tuple-element.8.y_ref, bf16[3,12,2,8,128,128]{5,4,3,2,1,0:T(8,128)(2,1)} %get-tuple-element.9.kv_hbm), custom_call_target="tpu_custom_call" | custom-call | flops 1000000 | bytes 30000000 | tf_op jit(solution)/shard_map/store/pallas_call | solution.py:686

commit v2 on v1

--- a/solution.py
+++ b/solution.py
@@ -538,7 +538,31 @@
         get_w_out().wait()
 
         @pl.loop(0, N_CHUNKS)
+        def _(chunk):
+            bs = pl.ds(chunk * nb, nb)
+
+            @pl.when(is_first)
+            def _():
+                drain(send.at[pl.ds(1, 2), bs, pl.ds(0, n - 1)], send_sem.at[chunk])
+                drain(near.at[:, bs], near_send_sem.at[chunk])
+
+            @pl.when(later_on)
+            def _():
+                drain(send.at[:, bs, pl.ds(0, n - 1)], send_sem.at[chunk])
+
+        def drain_ctx(chunk):
+            bs = pl.ds(chunk * nb, nb)
+
+            @pl.when(is_first)
+            def _():
+                drain(ctx_send.at[bs, pl.ds(0, n - FIRST)], ctx_send_sem.at[chunk])
+                drain(ctx_near.at[bs, 0], ctx_near_send_sem.at[chunk])
+
+            pl.when(later_on)(lambda: drain(ctx_send.at[bs, pl.ds(0, n - FIRST - 1)], ctx_send_sem.at[chunk]))
+
+        @pl.loop(0, N_CHUNKS)
         def _(turn):
+            pl.when(turn > 1)(lambda: drain_ctx(turn - 2))
             chunk = jnp.where(turn == 2, RELAYED, jnp.where((turn > 2) & (turn <= RELAYED), turn - 1, turn))
 
             g = pl.ds(pl.multiple_of(chunk * rows, rows), rows)
@@ -561,6 +585,14 @@
                         acc[g, cs] = total
                     else:
                         h_mlp[g, cs] = total.astype(BF16)
+
+        for chunk in (N_CHUNKS - 2, N_CHUNKS - 1):
+            drain_ctx(chunk)
+
+        @pl.when(is_first)
+        def _():
+            for chunk in range(RELAYED):
+                drain(relay.at[pl.ds(chunk * nb, nb)], relay_send_sem.at[chunk])
 
     pl.run_scoped(
         rest,
@@ -572,23 +604,6 @@
         pltpu.VMEM((3, nb, dests, heads, FIRST, seq_dev, head_dim), BF16),
         pltpu.VMEM((nb, FIRST, seq_dev, dests * cols), BF16),
     )
-
-    @pl.loop(0, N_CHUNKS)
-    def _(chunk):
-        bs = pl.ds(chunk * nb, nb)
-
-        @pl.when(is_first)
-        def _():
-            drain(send.at[pl.ds(1, 2), bs, pl.ds(0, n - 1)], send_sem.at[chunk])
-            drain(near.at[:, bs], near_send_sem.at[chunk])
-            drain(ctx_send.at[bs, pl.ds(0, n - FIRST)], ctx_send_sem.at[chunk])
-            drain(ctx_near.at[bs, 0], ctx_near_send_sem.at[chunk])
-            pl.when(chunk < RELAYED)(lambda: drain(relay.at[bs], relay_send_sem.at[chunk]))
-
-        @pl.when(later_on)
-        def _():
-            drain(send.at[:, bs, pl.ds(0, n - 1)], send_sem.at[chunk])
-            drain(ctx_send.at[bs, pl.ds(0, n - FIRST - 1)], ctx_send_sem.at[chunk])
 
 
 def store_kernel(y_ref, kv_hbm, y_hbm, k_hbm, v_hbm, buf, in_sem, out_sem, y_sem):
@@ -603,10 +618,11 @@
     ]
     for copy in get:
         copy.start()
+    for copy in get:
+        copy.wait()
     y_out.start()
-    for got, going in zip(get, put):
-        got.wait()
-        going.start()
+    for copy in put:
+        copy.start()
     for copy in put:
         copy.wait()
     y_out.wait()

time: 272 us -> 272 us (level)
  no operation moved by 1% of the time
where the time goes in v2:
time: 272 us
  Pallas kernels  271 us (100%)
    pallas_call x1, Pallas kernels, local_layer(): pl.pallas_call(functools.partial(layer_kernel, n), out_shape=[pltpu.VMEM(...  260 us
    pallas_call x1, Pallas kernels, local_layer(): pl.pallas_call(store_kernel, out_shape=[jax.ShapeDtypeStruct((rows, width...  11.4 us

profile of v2, /device:TPU:27, one launch (start us, length us, event | category | flops | bytes accessed | tf_op | source)
XLA Modules:
  0.0 271.8 jit_solution(14730663484576798779)
XLA Ops:
  0.6 259.8 %layer.1 = (bf16[1536,2048]{1,0:T(8,128)(2,1)S(1)}, bf16[3,12,2,8,128,128]{5,4,3,2,1,0:T(8,128)(2,1)}, bf16[3,12,8,2,128,128]{5,4,3,2,1,0:T(8,128)(2,1)}, bf16[1...) custom-call(bf16[1536,2048]{1,0:T(8,128)(2,1)} %bitcast.10, ...), custom_call_target="tpu_custom_call" | custom-call | flops 154618822656 | bytes 300000000 | tf_op jit(solution)/shard_map/layer/pallas_call | solution.py:646
  260.4 11.4 %store.1 = (bf16[1536,2048]{1,0:T(8,128)(2,1)}, bf16[12,2,8,128,128]{4,3,2,1,0:T(8,128)(2,1)}, bf16[12,2,8,128,128]{4,3,2,1,0:T(8,128)(2,1)}) custom-call(bf16[1536,2048]{1,0:T(8,128)(2,1)S(1)} %get-tuple-element.8.y_ref, bf16[3,12,2,8,128,128]{5,4,3,2,1,0:T(8,128)(2,1)} %get-tuple-element.9.kv_hbm), custom_call_target="tpu_custom_call" | custom-call | flops 1000000 | bytes 30000000 | tf_op jit(solution)/shard_map/store/pallas_call | solution.py:702

commit v3 on v2

--- a/solution.py
+++ b/solution.py
@@ -12,12 +12,13 @@
 ROPE_BASE = 10000.0
 LOG2E = 1.4426950408889634
 N_CHUNKS = 6
+UNITS = N_CHUNKS + 1
 UP_TILE = 512
 QKV_HEADS = 8
 Q_TILE = 256
 FIRST = 2
 LATE_STEPS = 2
-RELAYED = 4
+RELAYED = 5
 F32 = jnp.float32
 BF16 = jnp.bfloat16
 
@@ -106,27 +107,32 @@
     def peer(step):
         return lax.bitwise_xor(me, step)
 
-    def rows_of(chunk, first, count=1):
-        return ctx_rows.at[pl.ds(chunk * nb, nb), :, pl.ds(pl.multiple_of(first * cols, cols), count * cols)]
-
-    def put(chunk, kind, to, frm):
-        bs = pl.ds(chunk * nb, nb)
+    def rows_of(bs, first, count=1):
+        return ctx_rows.at[bs, :, pl.ds(pl.multiple_of(first * cols, cols), count * cols)]
+
+    half = nb // 2
+
+    def span(unit, small):
+        return pl.ds(n_batch - nb + (unit - (N_CHUNKS - 1)) * half, half) if small else pl.ds(unit * nb, nb)
+
+    def put(unit, kind, to, frm, small=False):
+        bs = span(unit, small)
         return pltpu.make_async_remote_copy(
             src_ref=send.at[kind, bs, to],
             dst_ref=recv.at[kind, bs, :, frm],
-            send_sem=send_sem.at[chunk],
-            recv_sem=recv_sem.at[chunk, kind],
+            send_sem=send_sem.at[unit],
+            recv_sem=recv_sem.at[unit, kind],
             device_id={"sp": to},
             device_id_type=pl.DeviceIdType.MESH,
         )
 
-    def put_ctx(chunk, to, frm):
-        bs = pl.ds(chunk * nb, nb)
+    def put_ctx(unit, to, frm, small=False):
+        bs = span(unit, small)
         return pltpu.make_async_remote_copy(
             src_ref=ctx_send.at[bs, to],
-            dst_ref=rows_of(chunk, frm),
-            send_sem=ctx_send_sem.at[chunk],
-            recv_sem=ctx_recv_sem.at[chunk, frm // FIRST],
+            dst_ref=rows_of(bs, frm),
+            send_sem=ctx_send_sem.at[unit],
+            recv_sem=ctx_recv_sem.at[unit, frm // FIRST],
             device_id={"sp": to},
             device_id_type=pl.DeviceIdType.MESH,
         )
@@ -146,7 +152,7 @@
         bs = pl.ds(chunk * nb, nb)
         return pltpu.make_async_remote_copy(
             src_ref=relay.at[bs, slot],
-            dst_ref=rows_of(chunk, 2 * FIRST + slot),
+            dst_ref=rows_of(bs, 2 * FIRST + slot),
             send_sem=relay_send_sem.at[chunk],
             recv_sem=ctx_recv_sem.at[chunk, 2],
             device_id={"sp": me + FIRST},
@@ -168,7 +174,7 @@
         bs = pl.ds(chunk * nb, nb)
         return pltpu.make_async_remote_copy(
             src_ref=ctx_near.at[bs, 1 - me],
-            dst_ref=rows_of(chunk, me * dests, dests),
+            dst_ref=rows_of(bs, me * dests, dests),
             send_sem=ctx_near_send_sem.at[chunk],
             recv_sem=ctx_near_recv_sem.at[chunk],
             device_id={"sp": 1 - me},
@@ -213,15 +219,20 @@
             dst = recv.at[kind, pl.ds(chunk * nb, nb), :, me]
             return pltpu.make_async_copy(own.at[kind], dst, own_sem.at[kind])
 
+        def send_unit(unit, block, small):
+            for d in range(dests):
+                to = lax.rem(block, parts) * dests + lax.rem(me + d, dests)
+
+                @pl.when((to != me) & jnp.logical_not(is_first & (block < parts)))
+                def _():
+                    put(unit, block // parts, to, me, small).start()
+
         def send_block(step):
             bounce(step).wait()
             block = lax.rem(step, blocks)
-            for d in range(dests):
-                to = lax.rem(block, parts) * dests + lax.rem(me + d, dests)
-
-                @pl.when((to != me) & jnp.logical_not(is_first & (block < parts)))
-                def _():
-                    put(step // blocks, block // parts, to, me).start()
+            is_last = step // blocks == N_CHUNKS - 1
+            pl.when(jnp.logical_not(is_last))(lambda: send_unit(step // blocks, block, False))
+            pl.when(is_last)(lambda: send_unit(N_CHUNKS - 1, block, True))
 
             @pl.when(is_first & (lax.rem(block, parts) == 1 - me))
             def _():
@@ -333,6 +344,7 @@
                 send_block(step - 1)
 
         send_block(N_CHUNKS * blocks - 1)
+        pl.loop(0, blocks)(lambda block: send_unit(UNITS - 1, block, True))
         for kind in range(3):
             put_own(N_CHUNKS - 1, kind).wait()
 
@@ -365,8 +377,10 @@
         def get_w_out():
             return pltpu.make_async_copy(w_out, w_buf, w_sem.at[0])
 
-        def get_qkv(chunk, kind):
-            return pltpu.make_async_copy(recv.at[kind, pl.ds(chunk * nb, nb)], qkv_buf.at[kind], qkv_sem.at[kind])
+        def get_qkv(unit, kind, small):
+            count = half if small else nb
+            to = qkv_buf.at[kind, pl.ds(0, count)]
+            return pltpu.make_async_copy(recv.at[kind, span(unit, small)], to, qkv_sem.at[kind])
 
         def get_own_near(chunk, kind):
             src = send.at[kind, pl.ds(chunk * nb, nb), pl.ds(me * dests, dests)]
@@ -376,30 +390,23 @@
             src = near.at[kind, pl.ds(chunk * nb, nb)]
             return pltpu.make_async_copy(src, both.at[kind, :, :, :, 1 - me], near_sem.at[kind, 1])
 
-        def bounce_ctx(chunk):
-            dst = ctx_send.at[pl.ds(chunk * nb, nb), pl.ds(FIRST, later)]
-            return pltpu.make_async_copy(ctx_buf, dst, bounce_sem.at[0])
+        def bounce_ctx(unit, small):
+            dst = ctx_send.at[span(unit, small), pl.ds(FIRST, later)]
+            return pltpu.make_async_copy(ctx_buf.at[pl.ds(0, half if small else nb)], dst, bounce_sem.at[0])
 
         def bounce_near(chunk):
             return pltpu.make_async_copy(near_buf, ctx_near.at[pl.ds(chunk * nb, nb)], bounce_sem.at[1])
 
-        def send_ctx(chunk):
-            bounce_ctx(chunk).wait()
-            relays = (me // FIRST == 2) & (chunk < RELAYED)
+        def send_ctx(unit, small=False):
+            bounce_ctx(unit, small).wait()
+            relays = (me // FIRST == 2) & (unit < RELAYED)
 
             def one(other):
-                if other // FIRST == 1:
-
-                    @pl.when(relays)
-                    def _():
-                        put_relay(chunk, other, me - 2 * FIRST).start()
-
-                    @pl.when(jnp.logical_not(relays))
-                    def _():
-                        put_ctx(chunk, other, me).start()
-
+                if other // FIRST == 1 and not small:
+                    pl.when(relays)(lambda: put_relay(unit, other, me - 2 * FIRST).start())
+                    pl.when(jnp.logical_not(relays))(lambda: put_ctx(unit, other, me).start())
                 else:
-                    put_ctx(chunk, other, me).start()
+                    put_ctx(unit, other, me, small).start()
 
             each_peer(one, FIRST)
 
@@ -412,32 +419,59 @@
             for slot in range(FIRST):
                 forward(chunk, slot).start()
 
-        def load_qkv(chunk):
+        def load_qkv(unit, small=False):
+            bs = span(unit, small)
             for kind in range(3):
-                got = lambda count: recv.at[kind, pl.ds(chunk * nb, nb), :, pl.ds(0, count)]
+                got = lambda count: recv.at[kind, bs, :, pl.ds(0, count)]
                 if kind:
-                    drain(got(n - 1), recv_sem.at[chunk, kind])
+                    drain(got(n - 1), recv_sem.at[unit, kind])
                 else:
-                    pl.when(is_first)(lambda: drain(got(n - FIRST), recv_sem.at[chunk, kind]))
-                    pl.when(later_on)(lambda: drain(got(n - FIRST - 1), recv_sem.at[chunk, kind]))
-                get_qkv(chunk, kind).start()
-
-            @pl.when(is_first)
-            def _():
-                drain(near.at[:, pl.ds(chunk * nb, nb)], near_recv_sem.at[chunk])
-                for kind in range(3):
-                    get_own_near(chunk, kind).start()
-                    get_other_near(chunk, kind).start()
+                    pl.when(is_first)(lambda: drain(got(n - FIRST), recv_sem.at[unit, kind]))
+                    pl.when(later_on)(lambda: drain(got(n - FIRST - 1), recv_sem.at[unit, kind]))
+                get_qkv(unit, kind, small).start()
+
+        def load_near(chunk):
+            drain(near.at[:, pl.ds(chunk * nb, nb)], near_recv_sem.at[chunk])
+            for kind in range(3):
+                get_own_near(chunk, kind).start()
+                get_other_near(chunk, kind).start()
+
+        def attend(unit, small=False):
+            for kind in range(3):
+                get_qkv(unit, kind, small).wait()
+            count = half if small else nb
+            for b in range(count):
+                for h in range(heads):
+                    q = qkv_buf[0, b, h, FIRST:].reshape(later * seq_dev, head_dim)
+                    k, v = (qkv_buf[t, b, h].reshape(n * seq_dev, head_dim) for t in (1, 2))
+                    per = Q_TILE // seq_dev
+
+                    def write(i, out):
+                        ctx_buf[b, i * per : (i + 1) * per, :, h * head_dim : (h + 1) * head_dim] = out.reshape(
+                            per, seq_dev, head_dim
+                        )
+
+                    causal_head(q, k, v, write)
+            bounce_ctx(unit, small).start()
+
+            @pl.when(later_on)
+            def _():
+                rows_of(span(unit, small), me)[...] = ctx_buf[:count, me - FIRST]
 
         get_up(0).start()
         get_down(0).start()
         get_w_out().start()
 
-        @pl.loop(0, N_CHUNKS + 1)
-        def _(chunk):
-            early = steps - LATE_STEPS
-            first = chunk * early // N_CHUNKS
-            last = jnp.where(chunk < N_CHUNKS, (chunk + 1) * early // N_CHUNKS, steps)
+        early = steps - LATE_STEPS
+
+        def mlp_end(turn):
+            whole = (turn + 1) * early // N_CHUNKS
+            return jnp.where(turn < N_CHUNKS - 1, whole, jnp.where(turn < UNITS, early - UNITS + 1 + turn, steps))
+
+        @pl.loop(0, UNITS + 1)
+        def _(unit):
+            first, last = jnp.where(unit > 0, mlp_end(unit - 1), 0), mlp_end(unit)
+            is_small = (unit == UNITS - 1) | (unit == UNITS - 2)
 
             @pl.loop(first, last)
             def _(f):
@@ -448,9 +482,14 @@
                     get_up(f + 1).start()
                     get_down(f + 1).start()
 
-                @pl.when((f == last - 1) & (chunk < N_CHUNKS - 1))
-                def _():
-                    load_qkv(chunk)
+                @pl.when((f == last - 1) & (unit < N_CHUNKS - 1))
+                def _():
+                    load_qkv(unit)
+                    pl.when(is_first)(lambda: load_near(unit))
+
+                @pl.when((f == last - 1) & (unit == UNITS - 2))
+                def _():
+                    load_qkv(unit, True)
 
                 get_up(f).wait()
                 get_down(f).wait()
@@ -460,60 +499,35 @@
                     hid = (0.5 * up * (1.0 + lax.erf(up * 0.5**0.5))).astype(BF16)
                     acc[rs, :] += jnp.dot(hid, down_buf[slot], preferred_element_type=F32)
 
-                @pl.when((f == first) & (chunk > 0))
-                def _():
-                    @pl.when(chunk < N_CHUNKS)
-                    def _():
-                        send_ctx(chunk - 1)
-
-                    @pl.when(is_first)
-                    def _():
-                        send_near(chunk - 1)
-
-                @pl.when(is_first & (chunk == N_CHUNKS))
-                def _():
-                    first_relay = 1 + (f - first) * 2
-
-                    @pl.loop(first_relay, jnp.minimum(jnp.where(f == steps - 1, RELAYED, first_relay + 2), RELAYED))
-                    def _(c):
-                        pass_on(c)
-
-            @pl.when(chunk < N_CHUNKS)
-            def _():
-                @pl.when(chunk == N_CHUNKS - 1)
-                def _():
-                    load_qkv(chunk)
-
-                for kind in range(3):
-                    get_qkv(chunk, kind).wait()
-                for b in range(nb):
-                    for h in range(heads):
-                        q = qkv_buf[0, b, h, FIRST:].reshape(later * seq_dev, head_dim)
-                        k, v = (qkv_buf[t, b, h].reshape(n * seq_dev, head_dim) for t in (1, 2))
-                        per = Q_TILE // seq_dev
-
-                        def write(i, out):
-                            ctx_buf[b, i * per : (i + 1) * per, :, h * head_dim : (h + 1) * head_dim] = out.reshape(
-                                per, seq_dev, head_dim
-                            )
-
-                        causal_head(q, k, v, write)
-                bounce_ctx(chunk).start()
-
-                @pl.when(later_on)
-                def _():
-                    rows_of(chunk, me)[...] = ctx_buf[:, me - FIRST]
-
-                @pl.when(chunk == N_CHUNKS - 1)
-                def _():
-                    send_ctx(chunk)
-
-                    @pl.when(is_first)
-                    def _():
-                        pass_on(0)
-
-                @pl.when(is_first)
-                def _():
+                @pl.when((f == first) & (unit > 0) & (unit < N_CHUNKS))
+                def _():
+                    send_ctx(unit - 1)
+                    pl.when(is_first)(lambda: send_near(unit - 1))
+
+                @pl.when(is_first & (unit == UNITS))
+                def _():
+                    pl.when(f == first)(lambda: send_near(N_CHUNKS - 1))
+                    pass_on(1 + 2 * (f - first))
+                    pl.when(f == first)(lambda: pass_on(2))
+
+            pl.when(unit < N_CHUNKS - 1)(lambda: attend(unit))
+            pl.when(unit == UNITS - 1)(lambda: load_qkv(unit, True))
+
+            @pl.when(is_small)
+            def _():
+                attend(unit, True)
+                send_ctx(unit, True)
+
+            @pl.when(is_first & (unit != UNITS - 2) & (unit < UNITS))
+            def _():
+                chunk = jnp.minimum(unit, N_CHUNKS - 1)
+
+                @pl.when(unit == UNITS - 1)
+                def _():
+                    pass_on(0)
+                    load_near(chunk)
+
+                if chunk is not None:
                     for kind in range(3):
                         get_own_near(chunk, kind).wait()
                         get_other_near(chunk, kind).wait()
@@ -533,64 +547,64 @@
                                 causal_head(q, k, v, write)
 
                     bounce_near(chunk).start()
-                    rows_of(chunk, me * dests, dests)[...] = near_buf[:, me]
+                    rows_of(pl.ds(chunk * nb, nb), me * dests, dests)[...] = near_buf[:, me]
 
         get_w_out().wait()
 
-        @pl.loop(0, N_CHUNKS)
-        def _(chunk):
-            bs = pl.ds(chunk * nb, nb)
-
-            @pl.when(is_first)
-            def _():
-                drain(send.at[pl.ds(1, 2), bs, pl.ds(0, n - 1)], send_sem.at[chunk])
-                drain(near.at[:, bs], near_send_sem.at[chunk])
-
-            @pl.when(later_on)
-            def _():
-                drain(send.at[:, bs, pl.ds(0, n - 1)], send_sem.at[chunk])
-
-        def drain_ctx(chunk):
-            bs = pl.ds(chunk * nb, nb)
-
-            @pl.when(is_first)
-            def _():
-                drain(ctx_send.at[bs, pl.ds(0, n - FIRST)], ctx_send_sem.at[chunk])
-                drain(ctx_near.at[bs, 0], ctx_near_send_sem.at[chunk])
-
-            pl.when(later_on)(lambda: drain(ctx_send.at[bs, pl.ds(0, n - FIRST - 1)], ctx_send_sem.at[chunk]))
+        def drain_qkv(unit, small=False):
+            bs = span(unit, small)
+            pl.when(is_first)(lambda: drain(send.at[pl.ds(1, 2), bs, pl.ds(0, n - 1)], send_sem.at[unit]))
+            pl.when(later_on)(lambda: drain(send.at[:, bs, pl.ds(0, n - 1)], send_sem.at[unit]))
+
+        def drain_ctx(unit, small=False):
+            bs = span(unit, small)
+            pl.when(is_first)(lambda: drain(ctx_send.at[bs, pl.ds(0, n - FIRST)], ctx_send_sem.at[unit]))
+            pl.when(later_on)(lambda: drain(ctx_send.at[bs, pl.ds(0, n - FIRST - 1)], ctx_send_sem.at[unit]))
+
+        pl.loop(0, N_CHUNKS - 1)(drain_qkv)
+        pl.loop(N_CHUNKS - 1, UNITS)(lambda unit: drain_qkv(unit, True))
 
         @pl.loop(0, N_CHUNKS)
         def _(turn):
             pl.when(turn > 1)(lambda: drain_ctx(turn - 2))
-            chunk = jnp.where(turn == 2, RELAYED, jnp.where((turn > 2) & (turn <= RELAYED), turn - 1, turn))
-
+            pl.when(is_first & (turn == 2))(lambda: pass_on(RELAYED - 1))
+            chunk = turn
             g = pl.ds(pl.multiple_of(chunk * rows, rows), rows)
             pl.when(is_first)(lambda: put_ctx_near(chunk).wait_recv())
             for part in range(n // FIRST):
                 home = me // FIRST
                 source = jnp.where(part == 0, home, jnp.where(part <= home, part - 1, part))
 
-                @pl.when(later_on)
-                def _():
-                    count = FIRST - (part == 0)
-                    drain(rows_of(chunk, 0, count), ctx_recv_sem.at[chunk, source])
-
-                span = pl.ds(pl.multiple_of(source * FIRST * cols, FIRST * cols), FIRST * cols)
-                left = ctx_rows[pl.ds(chunk * nb, nb), :, span].reshape(rows, FIRST * cols)
+                count = FIRST - (part == 0)
+
+                @pl.when(later_on & (chunk < N_CHUNKS - 1))
+                def _():
+                    drain(rows_of(span(chunk, False), 0, count), ctx_recv_sem.at[chunk, source])
+
+                @pl.when(later_on & (chunk == N_CHUNKS - 1))
+                def _():
+                    for unit in (N_CHUNKS - 1, N_CHUNKS):
+                        drain(rows_of(span(unit, True), 0, count), ctx_recv_sem.at[unit, source])
+
+                those = pl.ds(pl.multiple_of(source * FIRST * cols, FIRST * cols), FIRST * cols)
+                left = ctx_rows[pl.ds(chunk * nb, nb), :, those].reshape(rows, FIRST * cols)
                 for c in range(0, width, 1024):
                     cs = slice(c, c + 1024)
-                    total = acc[g, cs] + jnp.dot(left, w_buf[span, cs], preferred_element_type=F32)
+                    total = acc[g, cs] + jnp.dot(left, w_buf[those, cs], preferred_element_type=F32)
                     if part < n // FIRST - 1:
                         acc[g, cs] = total
                     else:
                         h_mlp[g, cs] = total.astype(BF16)
 
-        for chunk in (N_CHUNKS - 2, N_CHUNKS - 1):
-            drain_ctx(chunk)
+        drain_ctx(N_CHUNKS - 2)
+        pl.loop(N_CHUNKS - 1, UNITS)(lambda unit: drain_ctx(unit, True))
 
         @pl.when(is_first)
         def _():
+            for chunk in range(N_CHUNKS):
+                bs = pl.ds(chunk * nb, nb)
+                drain(near.at[:, bs], near_send_sem.at[chunk])
+                drain(ctx_near.at[bs, 0], ctx_near_send_sem.at[chunk])
             for chunk in range(RELAYED):
                 drain(relay.at[pl.ds(chunk * nb, nb)], relay_send_sem.at[chunk])
 
@@ -669,10 +683,10 @@
                 pltpu.SemaphoreType.DMA((2,)),
                 pltpu.SemaphoreType.DMA((3,)),
                 pltpu.SemaphoreType.DMA((3, 2)),
-                pltpu.SemaphoreType.DMA((N_CHUNKS,)),
-                pltpu.SemaphoreType.DMA((N_CHUNKS, 3)),
-                pltpu.SemaphoreType.DMA((N_CHUNKS,)),
-                pltpu.SemaphoreType.DMA((N_CHUNKS, n // FIRST)),
+                pltpu.SemaphoreType.DMA((UNITS,)),
+                pltpu.SemaphoreType.DMA((UNITS, 3)),
+                pltpu.SemaphoreType.DMA((UNITS,)),
+                pltpu.SemaphoreType.DMA((UNITS, n // FIRST)),
                 pltpu.SemaphoreType.DMA((N_CHUNKS,)),
                 pltpu.SemaphoreType.DMA((N_CHUNKS,)),
                 pltpu.SemaphoreType.DMA((N_CHUNKS,)),

time: 272 us -> 274 us (level)
  no operation moved by 1% of the time
where the time goes in v3:
time: 274 us
  Pallas kernels  273 us (100%)
    pallas_call x1, Pallas kernels, local_layer(): pl.pallas_call(functools.partial(layer_kernel, n), out_shape=[pltpu.VMEM(...  262 us
    pallas_call x1, Pallas kernels, local_layer(): pl.pallas_call(store_kernel, out_shape=[jax.ShapeDtypeStruct((rows, width...  11.4 us

profile of v3, /device:TPU:27, one launch (start us, length us, event | category | flops | bytes accessed | tf_op | source)
XLA Modules:
  0.0 274.0 jit_solution(11051537658026084162)
XLA Ops:
  0.6 262.0 %layer.1 = (bf16[1536,2048]{1,0:T(8,128)(2,1)S(1)}, bf16[3,12,2,8,128,128]{5,4,3,2,1,0:T(8,128)(2,1)}, bf16[3,12,8,2,128,128]{5,4,3,2,1,0:T(8,128)(2,1)}, bf16[1...) custom-call(bf16[1536,2048]{1,0:T(8,128)(2,1)} %bitcast.10, ...), custom_call_target="tpu_custom_call" | custom-call | flops 154618822656 | bytes 300000000 | tf_op jit(solution)/shard_map/layer/pallas_call | solution.py:660
  262.6 11.4 %store.1 = (bf16[1536,2048]{1,0:T(8,128)(2,1)}, bf16[12,2,8,128,128]{4,3,2,1,0:T(8,128)(2,1)}, bf16[12,2,8,128,128]{4,3,2,1,0:T(8,128)(2,1)}) custom-call(bf16[1536,2048]{1,0:T(8,128)(2,1)S(1)} %get-tuple-element.8.y_ref, bf16[3,12,2,8,128,128]{5,4,3,2,1,0:T(8,128)(2,1)} %get-tuple-element.9.kv_hbm), custom_call_target="tpu_custom_call" | custom-call | flops 1000000 | bytes 30000000 | tf_op jit(solution)/shard_map/store/pallas_call | solution.py:716

commit v4 on v3

--- a/solution.py
+++ b/solution.py
@@ -507,8 +507,7 @@
                 @pl.when(is_first & (unit == UNITS))
                 def _():
                     pl.when(f == first)(lambda: send_near(N_CHUNKS - 1))
-                    pass_on(1 + 2 * (f - first))
-                    pl.when(f == first)(lambda: pass_on(2))
+                    pass_on(2 + f - first)
 
             pl.when(unit < N_CHUNKS - 1)(lambda: attend(unit))
             pl.when(unit == UNITS - 1)(lambda: load_qkv(unit, True))
@@ -527,27 +526,27 @@
                     pass_on(0)
                     load_near(chunk)
 
-                if chunk is not None:
-                    for kind in range(3):
-                        get_own_near(chunk, kind).wait()
-                        get_other_near(chunk, kind).wait()
-
-                    @pl.loop(0, nb)
-                    def _(b):
-                        for d in range(dests):
-                            for h in range(heads):
-                                q, k, v = (both[t, b, d, h].reshape(Q_TILE, head_dim) for t in range(3))
-
-                                def write(i, out):
-                                    col = (d * heads + h) * head_dim
-                                    near_buf[b, :, :, col : col + head_dim] = out.reshape(
-                                        FIRST, seq_dev, head_dim
-                                    )
-
-                                causal_head(q, k, v, write)
-
-                    bounce_near(chunk).start()
-                    rows_of(pl.ds(chunk * nb, nb), me * dests, dests)[...] = near_buf[:, me]
+                for kind in range(3):
+                    get_own_near(chunk, kind).wait()
+                    get_other_near(chunk, kind).wait()
+
+                @pl.loop(0, nb)
+                def _(b):
+                    for d in range(dests):
+                        for h in range(heads):
+                            q, k, v = (both[t, b, d, h].reshape(Q_TILE, head_dim) for t in range(3))
+
+                            def write(i, out):
+                                col = (d * heads + h) * head_dim
+                                near_buf[b, :, :, col : col + head_dim] = out.reshape(
+                                    FIRST, seq_dev, head_dim
+                                )
+
+                            causal_head(q, k, v, write)
+
+                bounce_near(chunk).start()
+                rows_of(pl.ds(chunk * nb, nb), me * dests, dests)[...] = near_buf[:, me]
+                pl.when(unit == UNITS - 1)(lambda: pass_on(1))
 
         get_w_out().wait()
 

time: 274 us -> 274 us (level)
  no operation moved by 1% of the time
where the time goes in v4:
time: 274 us
  Pallas kernels  273 us (100%)
    pallas_call x1, Pallas kernels, local_layer(): pl.pallas_call(functools.partial(layer_kernel, n), out_shape=[pltpu.VMEM(...  262 us
    pallas_call x1, Pallas kernels, local_layer(): pl.pallas_call(store_kernel, out_shape=[jax.ShapeDtypeStruct((rows, width...  11.4 us

profile of v4, /device:TPU:27, one launch (start us, length us, event | category | flops | bytes accessed | tf_op | source)
XLA Modules:
  0.0 274.0 jit_solution(11580779501741981364)
XLA Ops:
  0.6 261.9 %layer.1 = (bf16[1536,2048]{1,0:T(8,128)(2,1)S(1)}, bf16[3,12,2,8,128,128]{5,4,3,2,1,0:T(8,128)(2,1)}, bf16[3,12,8,2,128,128]{5,4,3,2,1,0:T(8,128)(2,1)}, bf16[1...) custom-call(bf16[1536,2048]{1,0:T(8,128)(2,1)} %bitcast.10, ...), custom_call_target="tpu_custom_call" | custom-call | flops 154618822656 | bytes 300000000 | tf_op jit(solution)/shard_map/layer/pallas_call | solution.py:659
  262.5 11.4 %store.1 = (bf16[1536,2048]{1,0:T(8,128)(2,1)}, bf16[12,2,8,128,128]{4,3,2,1,0:T(8,128)(2,1)}, bf16[12,2,8,128,128]{4,3,2,1,0:T(8,128)(2,1)}) custom-call(bf16[1536,2048]{1,0:T(8,128)(2,1)S(1)} %get-tuple-element.8.y_ref, bf16[3,12,2,8,128,128]{5,4,3,2,1,0:T(8,128)(2,1)} %get-tuple-element.9.kv_hbm), custom_call_target="tpu_custom_call" | custom-call | flops 1000000 | bytes 30000000 | tf_op jit(solution)/shard_map/store/pallas_call | solution.py:715
